TPU v7x, 32 devices: a whole 2x2x4 slice. The times are simulated.
32 devices in a mesh: tm: 4 (over y, x), space: 8 (over z, core).
Axes of the slice: x: 2, y: 2, z: 4, core: 2. Of those that a mesh axis runs over, the one named last changes fastest.
Arguments:
- source: float32 [32, 512, 1024], P('tm', 'space'), may hold values from -6 to 6
- guess: float32 [32, 512, 1024], P('tm', 'space'), may hold values from -6 to 6
- start_state: float32 [512, 1024], P('space'), may hold values from -6 to 6
- conduct: float32 [512, 1024], P('space'), may hold values from 0.5 to 4
Outputs:
- solution_field: float32 [32, 512, 1024], P('tm', 'space')
- residual: float32 [32, 512, 1024], P('tm', 'space')
All inputs are finite; a program needn't handle non-finite values.
Results may differ from a plain program's by a relative error of at most 0.00002.
Values sent between devices are 32-bit elements; how exact they have to be, the bound alone decides.
A program may use at most 64 MiB of HBM per device.

v0:
```python
import functools

import jax
import jax.numpy as jnp
from jax import lax
from jax.experimental import pallas as pl
from jax.experimental.pallas import tpu as pltpu
from jax.sharding import PartitionSpec as P

damping = 0.8
MESH = pl.DeviceIdType.MESH
HALO = 8
LANES = 128

COND, F_GUESS, F_Q, F_E0, F_E1, F_E2, X_LATE, X_MID, X_EARLY = range(0, 18, 2)
T_GUESS, T_Q, T_E0, T_E1, T_E2, T_U3 = range(18, 24)
STEPS = 24


def kernel(
    tms, spaces, src_hbm, guess_hbm, start_hbm, cond_hbm, u3, rbuf,
    g, s, c, d, w, dk, wk, e, u1, er, ec, c0, c1, c2, u2, qbuf, fu,
    send_sem, recv_sem, load_sem,
):
    t = lax.axis_index("tm")
    z = lax.axis_index("space")
    has_up, has_dn = z > 0, z < spaces - 1
    has_before, has_after = t > 0, t < tms - 1
    steps, rows, cols = src_hbm.shape
    half = steps // 2
    full = rows + 2 * HALO
    mid = slice(HALO, HALO + rows)
    top, bot = slice(0, HALO), slice(HALO + rows, full)
    top_in, bot_in = slice(HALO, 2 * HALO), slice(rows, HALO + rows)
    chunks = cols // LANES
    later = slice(1, steps + 1)

    def remote(src, dst, k, dev):
        return pltpu.make_async_remote_copy(
            src_ref=src, dst_ref=dst, send_sem=send_sem.at[k], recv_sem=recv_sem.at[k],
            device_id=dev, device_id_type=MESH)

    up, dn = {"space": z - 1}, {"space": z + 1}
    sent = []

    class Edge:
        def __init__(self, k, first, last, halo_top, halo_bot):
            self.k, self.first, self.last, self.top, self.bot = k, first, last, halo_top, halo_bot

        def start(self):
            @pl.when(has_up)
            def _():
                remote(self.first, self.bot, self.k, up).start()

            @pl.when(has_dn)
            def _():
                remote(self.last, self.top, self.k + 1, dn).start()
            sent.append(self)

        def wait_recv(self):
            @pl.when(has_dn)
            def _():
                remote(self.first, self.bot, self.k, dn).wait_recv()

            @pl.when(has_up)
            def _():
                remote(self.last, self.top, self.k + 1, up).wait_recv()

        def wait_send(self):
            @pl.when(has_up)
            def _():
                remote(self.first, self.bot, self.k, up).wait_send()

            @pl.when(has_dn)
            def _():
                remote(self.last, self.top, self.k + 1, dn).wait_send()

    class Along:
        def __init__(self, k, src, dst):
            self.k, self.src, self.dst = k, src, dst

        def start(self):
            @pl.when(has_after)
            def _():
                remote(self.src, self.dst, self.k, {"tm": t + 1}).start()
            if self not in sent:
                sent.append(self)

        def wait_recv(self):
            @pl.when(has_before)
            def _():
                remote(self.src, self.dst, self.k, {"tm": t - 1}).wait_recv()

        def wait_send(self):
            @pl.when(has_after)
            def _():
                remote(self.src, self.dst, self.k, {"tm": t + 1}).wait_send()

    def within(k, ref, sl):
        return Edge(k, ref.at[sl, top_in], ref.at[sl, bot_in], ref.at[sl, top], ref.at[sl, bot])

    barrier = pltpu.get_barrier_semaphore()
    for flag, dev in ((has_up, up), (has_dn, dn), (has_before, {"tm": t - 1}), (has_after, {"tm": t + 1})):
        @pl.when(flag)
        def _(dev=dev):
            pl.semaphore_signal(barrier, inc=1, device_id=dev, device_id_type=MESH)

    loads = [
        pltpu.make_async_copy(cond_hbm, c.at[mid], load_sem.at[0]),
        pltpu.make_async_copy(guess_hbm, g.at[later, mid], load_sem.at[1]),
        pltpu.make_async_copy(src_hbm, s.at[later, mid], load_sem.at[2]),
    ]
    for load in loads:
        load.start()
    start_g = pltpu.make_async_copy(start_hbm, g.at[0, mid], load_sem.at[3])
    start_u = pltpu.make_async_copy(start_hbm, fu, load_sem.at[4])

    @pl.when(jnp.logical_not(has_before))
    def _():
        start_g.start()
        start_u.start()
        s[0, mid] = jnp.zeros((rows, cols), jnp.float32)
        for ref in (c0, c1, c2):
            ref[0, mid] = jnp.zeros((rows, cols), jnp.float32)

    for flag, edge in ((has_up, top), (has_dn, bot)):
        @pl.when(jnp.logical_not(flag))
        def _(edge=edge):
            c[edge] = jnp.zeros((HALO, cols), jnp.float32)
            for ref in (g, s, c0, c1, c2):
                if ref is g or ref is s or ref is c2:
                    ref[:, edge] = jnp.zeros((ref.shape[0], HALO, cols), jnp.float32)
                else:
                    ref[0, edge] = jnp.zeros((HALO, cols), jnp.float32)

    peers = sum(jnp.where(flag, 1, 0) for flag in (has_up, has_dn, has_before, has_after))
    pl.semaphore_wait(barrier, peers)

    along = Along(T_GUESS, guess_hbm.at[steps - 1], g.at[0, mid])
    along.start()
    a_guess = along
    x_cond = Edge(COND, cond_hbm.at[0:HALO], cond_hbm.at[rows - HALO : rows], c.at[top], c.at[bot])
    def halo(n, hbm, ref, k):
        return Edge(k, hbm.at[n - 1, 0:HALO], hbm.at[n - 1, rows - HALO : rows], ref.at[n, top], ref.at[n, bot])

    def guess_halo(n):
        return halo(n, guess_hbm, g, STEPS + 2 * (n - 1))

    def source_halo(n):
        return halo(n, src_hbm, s, STEPS + 2 * steps + 2 * (n - 1))

    x_cond.start()
    guess_halo(steps).start()
    for n in range(steps - 1, 0, -1):
        guess_halo(n).start()
        source_halo(n + 1).start()
    source_halo(1).start()
    for load in loads:
        load.wait()

    lane = lax.broadcasted_iota(jnp.int32, (full, LANES), 1)
    is_first, is_last = lane == 0, lane == LANES - 1

    def at(j):
        return slice(j * LANES, (j + 1) * LANES)

    def each(low, high, body):
        def step(i, carry):
            body(i)
            return carry
        lax.fori_loop(low, high, step, 0)

    def stencil(get, put):
        zero = jnp.zeros((full, LANES), jnp.float32)
        before, now = zero, get(0)
        for j in range(chunks):
            after = get(j + 1) if j + 1 < chunks else zero
            left = pltpu.roll(jnp.where(is_last, before, now), 1, 1)
            right = pltpu.roll(jnp.where(is_first, after, now), LANES - 1, 1)
            rim = (left + right) + (pltpu.roll(now, 1, 0) + pltpu.roll(now, full - 1, 0))
            put(j, now, rim)
            before, now = now, after

    def first_sweep(field, n, has_prev=True):
        def put(j, now, rim):
            drive = s[n, :, at(j)]
            if has_prev:
                drive = drive + field[n - 1, :, at(j)]
            e[n, :, at(j)] = d[:, at(j)] * drive + w[:, at(j)] * rim - now
        stencil(lambda j: field[n, :, at(j)], put)

    def second_sweep(field, errs, n, dst, weight, damp, inner=False):
        def put(j, now, rim):
            gain = damp * (now + weight[:, at(j)] * rim)
            if inner:
                dst[n, mid, at(j)] = field[n, mid, at(j)] + gain[mid]
            elif field is None:
                dst[n, :, at(j)] = gain
            else:
                dst[n, :, at(j)] = field[n, :, at(j)] + gain
        stencil(lambda j: errs[n, :, at(j)], put)

    def restrict(m):
        a, b = 2 * m - 1, 2 * m

        def put(j, now, rim):
            cc = c[:, at(j)]
            drive = (s[a, :, at(j)] + s[b, :, at(j)]) + (u1[a - 1, :, at(j)] + u1[a, :, at(j)])
            er[m, :, at(j)] = dk[:, at(j)] * (drive - now + cc * (rim - 4.0 * now))
        stencil(lambda j: u1[a, :, at(j)] + u1[b, :, at(j)], put)

    def coarse_defect(field, m):
        def put(j, now, rim):
            ec[m, :, at(j)] = er[m, :, at(j)] + dk[:, at(j)] * field[m - 1, :, at(j)] + wk[:, at(j)] * rim - now
        stencil(lambda j: field[m, :, at(j)], put)

    def sweep_one(low, high):
        each(low, high, lambda m: coarse_defect(c0, m))
        each(low, high, lambda m: second_sweep(c0, ec, m, c1, wk, damping))

    def sweep_two(low, high):
        each(low, high, lambda m: coarse_defect(c1, m))
        each(low, high, lambda m: second_sweep(c1, ec, m, c2, wk, damping, inner=True))

    def prolong(m):
        for j in range(chunks):
            u2[2 * m, :, at(j)] = u1[2 * m, :, at(j)] + c2[m, :, at(j)]
            u2[2 * m - 1, :, at(j)] = u1[2 * m - 1, :, at(j)] + 0.5 * (c2[m - 1, :, at(j)] + c2[m, :, at(j)])

    def last_residual(n, has_prev=True):
        def put(j, now, rim):
            flow = c[:, at(j)] * (rim - 4.0 * now) - now
            drive = s[n, mid, at(j)]
            if has_prev:
                drive = drive + u3[n - 1, mid, at(j)]
            rbuf[n - 1, :, at(j)] = flow[mid] + drive
        stencil(lambda j: u3[n, :, at(j)], put)

    for j in range(chunks):
        qbuf[:, at(j)] = s[steps, mid, at(j)] + g[steps - 1, mid, at(j)]
    a_q = Along(T_Q, qbuf, s.at[0, mid])
    a_e0 = Along(T_E0, c0.at[half, mid], c0.at[0, mid])
    a_e1 = Along(T_E1, c1.at[half, mid], c1.at[0, mid])
    a_e2 = Along(T_E2, c2.at[half, mid], c2.at[0, mid])
    a_u3 = Along(T_U3, u3.at[steps, mid], fu)

    x_cond.wait_recv()
    for j in range(chunks):
        cc = c[:, at(j)]
        dd = 1.0 / (1.0 + 4.0 * cc)
        dd2 = 1.0 / (1.0 + 8.0 * cc)
        d[:, at(j)], w[:, at(j)] = dd, cc * dd
        dk[:, at(j)], wk[:, at(j)] = dd2, 2.0 * cc * dd2
    a_q.start()
    guess_halo(steps).wait_recv()

    def local_step(i):
        n = steps - i
        guess_halo(n - 1).wait_recv()
        source_halo(n).wait_recv()

        @pl.when(i == 3)
        def _():
            a_e0.start()
        first_sweep(g, n)
        second_sweep(g, e, n, u1, w, damping)

        @pl.when(jnp.logical_and(lax.rem(i, 2) == 0, i > 0))
        def _():
            m = half + 1 - i // 2
            restrict(m)
            second_sweep(None, er, m, c0, wk, damping)

    each(0, steps - 1, local_step)

    @pl.when(jnp.logical_not(has_before))
    def _():
        start_g.wait()
        start_u.wait()
    a_guess.wait_recv()
    f_guess = within(F_GUESS, g, slice(0, 1))
    f_guess.start()
    sweep_one(3, half + 1)
    each(4, half + 1, lambda m: coarse_defect(c1, m))
    a_e1.start()
    each(4, half + 1, lambda m: second_sweep(c1, ec, m, c2, wk, damping, inner=True))
    f_guess.wait_recv()
    source_halo(1).wait_recv()
    each(1, 2, lambda n: first_sweep(g, n))
    a_e2.start()
    each(1, 2, lambda n: second_sweep(g, e, n, u1, w, damping))
    a_q.wait_recv()
    f_q = within(F_Q, s, slice(0, 1))
    f_q.start()
    f_q.wait_recv()
    each(0, 1, lambda n: first_sweep(g, n, has_prev=False))
    damp0 = jnp.where(has_before, damping, 0.0).astype(jnp.float32)
    each(0, 1, lambda n: second_sweep(g, e, n, u1, w, damp0))
    each(1, 2, restrict)
    each(1, 2, lambda m: second_sweep(None, er, m, c0, wk, damping))
    sweep_one(2, 3)
    sweep_two(3, 4)
    x_late = within(X_LATE, c2, slice(3, half + 1))
    x_late.start()
    a_e0.wait_recv()
    f_e0 = within(F_E0, c0, slice(0, 1))
    f_e0.start()
    x_late.wait_recv()
    each(half, half + 1, prolong)
    each(steps, steps + 1, lambda n: first_sweep(u2, n))
    each(steps, steps + 1, lambda n: second_sweep(u2, e, n, u3, w, damping))

    f_e0.wait_recv()
    each(1, 2, lambda m: coarse_defect(c0, m))
    a_u3.start()
    each(1, 2, lambda m: second_sweep(c0, ec, m, c1, wk, damping))
    sweep_two(2, 3)
    x_mid = within(X_MID, c2, slice(2, 3))
    x_mid.start()
    for j in range(chunks):
        u2[steps - 2, :, at(j)] = u1[steps - 2, :, at(j)] + c2[half - 1, :, at(j)]
    each(steps - 1, steps, lambda n: first_sweep(u2, n))
    each(steps - 1, steps, lambda n: second_sweep(u2, e, n, u3, w, damping))
    each(steps, steps + 1, last_residual)
    x_mid.wait_recv()
    each(3, half, prolong)
    for j in range(chunks):
        u2[4, :, at(j)] = u1[4, :, at(j)] + c2[2, :, at(j)]
    each(5, steps - 1, lambda n: first_sweep(u2, n))
    a_e1.wait_recv()
    f_e1 = within(F_E1, c1, slice(0, 1))
    f_e1.start()
    each(5, steps - 1, lambda n: second_sweep(u2, e, n, u3, w, damping))
    f_e1.wait_recv()
    sweep_two(1, 2)
    x_early = within(X_EARLY, c2, slice(1, 2))
    x_early.start()
    each(6, steps, last_residual)
    x_early.wait_recv()
    for j in range(chunks):
        u2[2, :, at(j)] = u1[2, :, at(j)] + c2[1, :, at(j)]
        u2[3, :, at(j)] = u1[3, :, at(j)] + 0.5 * (c2[1, :, at(j)] + c2[2, :, at(j)])
    each(3, 5, lambda n: first_sweep(u2, n))
    a_e2.wait_recv()
    f_e2 = within(F_E2, c2, slice(0, 1))
    f_e2.start()
    each(3, 5, lambda n: second_sweep(u2, e, n, u3, w, damping))
    each(4, 6, last_residual)
    f_e2.wait_recv()
    for j in range(chunks):
        u2[0, :, at(j)] = u1[0, :, at(j)] + c2[0, :, at(j)]
        u2[1, :, at(j)] = u1[1, :, at(j)] + 0.5 * (c2[0, :, at(j)] + c2[1, :, at(j)])
    each(1, 3, lambda n: first_sweep(u2, n))
    each(1, 3, lambda n: second_sweep(u2, e, n, u3, w, damping))
    each(2, 4, last_residual)
    each(1, 2, lambda n: last_residual(n, has_prev=False))
    for copy in sent:
        copy.wait_send()
    a_u3.wait_recv()
    rbuf[0] = rbuf[0] + fu[...]


def store(u3, rbuf, u_out, r_out, sem):
    steps, rows, _ = u_out.shape
    copies = [
        pltpu.make_async_copy(u3.at[1 : steps + 1, HALO : HALO + rows], u_out, sem.at[0]),
        pltpu.make_async_copy(rbuf, r_out, sem.at[1]),
    ]
    for copy in copies:
        copy.start()
    for copy in copies:
        copy.wait()


def solution(mesh):
    tms, spaces = mesh.shape["tm"], mesh.shape["space"]

    def shards(source, guess, start_state, conduct):
        steps, rows, cols = source.shape
        full, half = rows + 2 * HALO, steps // 2

        def buf(*lead):
            return pltpu.VMEM(lead + (full, cols), jnp.float32)

        fields = pl.pallas_call(
            functools.partial(kernel, tms, spaces),
            out_shape=(buf(steps + 1), pltpu.VMEM(source.shape, jnp.float32)),
            in_specs=[pl.BlockSpec(memory_space=pltpu.HBM)] * 4,
            out_specs=[pl.BlockSpec(memory_space=pltpu.VMEM)] * 2,
            scratch_shapes=[
                buf(steps + 1), buf(steps + 1), buf(), buf(), buf(), buf(), buf(),
                buf(steps + 1), buf(steps + 1), buf(half + 1), buf(half + 1),
                buf(half + 1), buf(half + 1), buf(half + 1), buf(steps + 1),
                pltpu.VMEM((rows, cols), jnp.float32),
                pltpu.VMEM((rows, cols), jnp.float32),
                pltpu.SemaphoreType.DMA((STEPS + 4 * steps,)),
                pltpu.SemaphoreType.DMA((STEPS + 4 * steps,)),
                pltpu.SemaphoreType.DMA((5,)),
            ],
            compiler_params=pltpu.CompilerParams(
                collective_id=0, has_side_effects=True, vmem_limit_bytes=59 * 1024 * 1024),
        )(source, guess, start_state, conduct)
        return pl.pallas_call(
            store,
            out_shape=(jax.ShapeDtypeStruct(source.shape, jnp.float32),) * 2,
            in_specs=[pl.BlockSpec(memory_space=pltpu.VMEM)] * 2,
            out_specs=[pl.BlockSpec(memory_space=pl.ANY)] * 2,
            scratch_shapes=[pltpu.SemaphoreType.DMA((2,))],
            compiler_params=pltpu.CompilerParams(vmem_limit_bytes=8 * 1024 * 1024),
        )(*fields)

    return jax.shard_map(
        shards,
        mesh=mesh,
        in_specs=(P("tm", "space", None), P("tm", "space", None), P("space", None), P("space", None)),
        out_specs=(P("tm", "space", None), P("tm", "space", None)),
        check_vma=False,
    )
```

profile of v0, /device:TPU:5, one launch (start us, length us, event | category | flops | bytes accessed | tf_op | source)
XLA Modules:
  0.0 43.8 jit_solution(4655452992503361470)
XLA Ops:
  0.6 41.1 %shard_map.59 = (f32[9,80,1024]{2,1,0:T(8,128)S(1)}, f32[8,64,1024]{2,1,0:T(8,128)S(1)}) custom-call(f32[8,64,1024]{2,1,0:T(8,128)} %src_hbm.1, f32[8,64,1024]{2,1,0:T(8,128)} %guess_hbm.1, f32[64,1024]{1,0:T(8,128)} %start_hbm.1, f32[64,1024]{1,0:T(8,128)} %cond_hbm.1), custom_call_target="tpu_custom_call" | custom-call | tf_op jit(solution)/shard_map/pallas_call | solution.py:385
  41.8 2.0 %shard_map.60 = (f32[8,64,1024]{2,1,0:T(8,128)}, f32[8,64,1024]{2,1,0:T(8,128)}) custom-call(f32[9,80,1024]{2,1,0:T(8,128)S(1)} %get-tuple-element.4.u3, f32[8,64,1024]{2,1,0:T(8,128)S(1)} %get-tuple-element.5.rbuf), custom_call_target="tpu_custom_call" | custom-call | tf_op jit(solution)/shard_map/pallas_call | solution.py:403
where the time goes:
time: 43.9 us; the launch traced here: 43.8 us
  Pallas kernels  43.1 us (98%)
  between operations  0.64 us (1%)
    pallas_call x1, Pallas kernels, shards(): pl.pallas_call(functools.partial(kernel, tms, spaces), out_shape=(buf(ste...  41.1 us
    pallas_call x1, Pallas kernels, shards(): pl.pallas_call(store, out_shape=(jax.ShapeDtypeStruct(source.shape, jnp.f...  2.03 us

commit v1 on v0

--- a/solution.py
+++ b/solution.py
@@ -322,28 +322,28 @@
     each(steps - 1, steps, lambda n: first_sweep(u2, n))
     each(steps - 1, steps, lambda n: second_sweep(u2, e, n, u3, w, damping))
     each(steps, steps + 1, last_residual)
-    x_mid.wait_recv()
-    each(3, half, prolong)
-    for j in range(chunks):
-        u2[4, :, at(j)] = u1[4, :, at(j)] + c2[2, :, at(j)]
-    each(5, steps - 1, lambda n: first_sweep(u2, n))
     a_e1.wait_recv()
     f_e1 = within(F_E1, c1, slice(0, 1))
     f_e1.start()
+    x_mid.wait_recv()
+    each(3, half, prolong)
+    for j in range(chunks):
+        u2[4, :, at(j)] = u1[4, :, at(j)] + c2[2, :, at(j)]
+    each(5, steps - 1, lambda n: first_sweep(u2, n))
     each(5, steps - 1, lambda n: second_sweep(u2, e, n, u3, w, damping))
     f_e1.wait_recv()
     sweep_two(1, 2)
     x_early = within(X_EARLY, c2, slice(1, 2))
     x_early.start()
     each(6, steps, last_residual)
+    a_e2.wait_recv()
+    f_e2 = within(F_E2, c2, slice(0, 1))
+    f_e2.start()
     x_early.wait_recv()
     for j in range(chunks):
         u2[2, :, at(j)] = u1[2, :, at(j)] + c2[1, :, at(j)]
         u2[3, :, at(j)] = u1[3, :, at(j)] + 0.5 * (c2[1, :, at(j)] + c2[2, :, at(j)])
     each(3, 5, lambda n: first_sweep(u2, n))
-    a_e2.wait_recv()
-    f_e2 = within(F_E2, c2, slice(0, 1))
-    f_e2.start()
     each(3, 5, lambda n: second_sweep(u2, e, n, u3, w, damping))
     each(4, 6, last_residual)
     f_e2.wait_recv()

time: 43.9 us -> 42.3 us (0.964)
  Pallas kernels: 43.1 us -> 41.5 us
    pallas_call x1, Pallas kernels: 41.1 us -> 39.5 us  [shards(): pl.pallas_call(functools.partial(kernel, tms, spaces), out_shape=(buf(ste...]
where the time goes in v1:
time: 42.3 us; the launch traced here: 42.1 us
  Pallas kernels  41.5 us (98%)
  between operations  0.64 us (2%)
    pallas_call x1, Pallas kernels, shards(): pl.pallas_call(functools.partial(kernel, tms, spaces), out_shape=(buf(ste...  39.5 us
    pallas_call x1, Pallas kernels, shards(): pl.pallas_call(store, out_shape=(jax.ShapeDtypeStruct(source.shape, jnp.f...  2.03 us

profile of v1, /device:TPU:5, one launch (start us, length us, event | category | flops | bytes accessed | tf_op | source)
XLA Modules:
  0.0 42.1 jit_solution(1876318006519013664)
XLA Ops:
  0.6 39.5 %shard_map.59 = (f32[9,80,1024]{2,1,0:T(8,128)S(1)}, f32[8,64,1024]{2,1,0:T(8,128)S(1)}) custom-call(f32[8,64,1024]{2,1,0:T(8,128)} %src_hbm.1, f32[8,64,1024]{2,1,0:T(8,128)} %guess_hbm.1, f32[64,1024]{1,0:T(8,128)} %start_hbm.1, f32[64,1024]{1,0:T(8,128)} %cond_hbm.1), custom_call_target="tpu_custom_call" | custom-call | tf_op jit(solution)/shard_map/pallas_call | solution.py:385
  40.1 2.0 %shard_map.60 = (f32[8,64,1024]{2,1,0:T(8,128)}, f32[8,64,1024]{2,1,0:T(8,128)}) custom-call(f32[9,80,1024]{2,1,0:T(8,128)S(1)} %get-tuple-element.4.u3, f32[8,64,1024]{2,1,0:T(8,128)S(1)} %get-tuple-element.5.rbuf), custom_call_target="tpu_custom_call" | custom-call | tf_op jit(solution)/shard_map/pallas_call | solution.py:403

commit v2 on v1

--- a/solution.py
+++ b/solution.py
@@ -12,9 +12,9 @@
 HALO = 8
 LANES = 128
 
-COND, F_GUESS, F_Q, F_E0, F_E1, F_E2, X_LATE, X_MID, X_EARLY = range(0, 18, 2)
-T_GUESS, T_Q, T_E0, T_E1, T_E2, T_U3 = range(18, 24)
-STEPS = 24
+EARLY, SPACE, ALONG = range(0, 6, 2)
+T_GUESS, T_Q, T_E0, T_E1, T_E2, T_U3 = range(6)
+SETS, PLANES = 4, 6
 
 
 def kernel(
@@ -35,69 +35,71 @@
     chunks = cols // LANES
     later = slice(1, steps + 1)
 
-    def remote(src, dst, k, dev):
+    def remote(src, dst, sent, k, dev):
         return pltpu.make_async_remote_copy(
-            src_ref=src, dst_ref=dst, send_sem=send_sem.at[k], recv_sem=recv_sem.at[k],
+            src_ref=src, dst_ref=dst, send_sem=send_sem.at[sent], recv_sem=recv_sem.at[k],
             device_id=dev, device_id_type=MESH)
 
     up, dn = {"space": z - 1}, {"space": z + 1}
-    sent = []
+    first_set = 2 * half
+    first_plane = first_set + 2 * SETS
 
     class Edge:
-        def __init__(self, k, first, last, halo_top, halo_bot):
-            self.k, self.first, self.last, self.top, self.bot = k, first, last, halo_top, halo_bot
+        def __init__(self, sent, k, first, last, halo_top, halo_bot):
+            self.sent, self.k, self.first, self.last, self.top, self.bot = sent, k, first, last, halo_top, halo_bot
 
         def start(self):
             @pl.when(has_up)
             def _():
-                remote(self.first, self.bot, self.k, up).start()
+                remote(self.first, self.bot, self.sent, self.k, up).start()
 
             @pl.when(has_dn)
             def _():
-                remote(self.last, self.top, self.k + 1, dn).start()
-            sent.append(self)
+                remote(self.last, self.top, self.sent + 1, self.k + 1, dn).start()
 
         def wait_recv(self):
             @pl.when(has_dn)
             def _():
-                remote(self.first, self.bot, self.k, dn).wait_recv()
+                remote(self.first, self.bot, self.sent, self.k, dn).wait_recv()
 
             @pl.when(has_up)
             def _():
-                remote(self.last, self.top, self.k + 1, up).wait_recv()
+                remote(self.last, self.top, self.sent + 1, self.k + 1, up).wait_recv()
 
         def wait_send(self):
             @pl.when(has_up)
             def _():
-                remote(self.first, self.bot, self.k, up).wait_send()
+                remote(self.first, self.bot, self.sent, self.k, up).wait_send()
 
             @pl.when(has_dn)
             def _():
-                remote(self.last, self.top, self.k + 1, dn).wait_send()
+                remote(self.last, self.top, self.sent + 1, self.k + 1, dn).wait_send()
 
     class Along:
         def __init__(self, k, src, dst):
-            self.k, self.src, self.dst = k, src, dst
+            self.k, self.src, self.dst = first_plane + k, src, dst
 
         def start(self):
             @pl.when(has_after)
             def _():
-                remote(self.src, self.dst, self.k, {"tm": t + 1}).start()
-            if self not in sent:
-                sent.append(self)
+                remote(self.src, self.dst, ALONG, self.k, {"tm": t + 1}).start()
 
         def wait_recv(self):
             @pl.when(has_before)
             def _():
-                remote(self.src, self.dst, self.k, {"tm": t - 1}).wait_recv()
+                remote(self.src, self.dst, ALONG, self.k, {"tm": t - 1}).wait_recv()
 
         def wait_send(self):
             @pl.when(has_after)
             def _():
-                remote(self.src, self.dst, self.k, {"tm": t + 1}).wait_send()
-
-    def within(k, ref, sl):
-        return Edge(k, ref.at[sl, top_in], ref.at[sl, bot_in], ref.at[sl, top], ref.at[sl, bot])
+                remote(self.src, self.dst, ALONG, self.k, {"tm": t + 1}).wait_send()
+
+    def within(turn, ref, sl):
+        return Edge(SPACE, first_set + 2 * turn, ref.at[sl, top_in], ref.at[sl, bot_in], ref.at[sl, top], ref.at[sl, bot])
+
+    def tiles(sent, k, count):
+        ref = s.at[0:1, 0 : count * HALO] if count * HALO <= full else s.at[0:2, 0 : count * HALO // 2]
+        return Edge(sent, k, ref, ref, ref, ref)
 
     barrier = pltpu.get_barrier_semaphore()
     for flag, dev in ((has_up, up), (has_dn, dn), (has_before, {"tm": t - 1}), (has_after, {"tm": t + 1})):
@@ -105,15 +107,17 @@
         def _(dev=dev):
             pl.semaphore_signal(barrier, inc=1, device_id=dev, device_id_type=MESH)
 
+    last_guess = pltpu.make_async_copy(guess_hbm.at[steps - 1], g.at[steps, mid], load_sem.at[0])
+    last_guess.start()
     loads = [
-        pltpu.make_async_copy(cond_hbm, c.at[mid], load_sem.at[0]),
-        pltpu.make_async_copy(guess_hbm, g.at[later, mid], load_sem.at[1]),
+        pltpu.make_async_copy(cond_hbm, c.at[mid], load_sem.at[1]),
         pltpu.make_async_copy(src_hbm, s.at[later, mid], load_sem.at[2]),
+        pltpu.make_async_copy(guess_hbm.at[0 : steps - 1], g.at[1:steps, mid], load_sem.at[3]),
     ]
     for load in loads:
         load.start()
-    start_g = pltpu.make_async_copy(start_hbm, g.at[0, mid], load_sem.at[3])
-    start_u = pltpu.make_async_copy(start_hbm, fu, load_sem.at[4])
+    start_g = pltpu.make_async_copy(start_hbm, g.at[0, mid], load_sem.at[4])
+    start_u = pltpu.make_async_copy(start_hbm, fu, load_sem.at[5])
 
     @pl.when(jnp.logical_not(has_before))
     def _():
@@ -136,25 +140,20 @@
     peers = sum(jnp.where(flag, 1, 0) for flag in (has_up, has_dn, has_before, has_after))
     pl.semaphore_wait(barrier, peers)
 
-    along = Along(T_GUESS, guess_hbm.at[steps - 1], g.at[0, mid])
-    along.start()
-    a_guess = along
-    x_cond = Edge(COND, cond_hbm.at[0:HALO], cond_hbm.at[rows - HALO : rows], c.at[top], c.at[bot])
-    def halo(n, hbm, ref, k):
-        return Edge(k, hbm.at[n - 1, 0:HALO], hbm.at[n - 1, rows - HALO : rows], ref.at[n, top], ref.at[n, bot])
-
-    def guess_halo(n):
-        return halo(n, guess_hbm, g, STEPS + 2 * (n - 1))
-
-    def source_halo(n):
-        return halo(n, src_hbm, s, STEPS + 2 * steps + 2 * (n - 1))
-
-    x_cond.start()
-    guess_halo(steps).start()
-    for n in range(steps - 1, 0, -1):
-        guess_halo(n).start()
-        source_halo(n + 1).start()
-    source_halo(1).start()
+    a_guess = Along(T_GUESS, g.at[steps, mid], g.at[0, mid])
+    last_guess.wait()
+    a_guess.start()
+
+    def halo(group, n, hbm, ref):
+        Edge(EARLY, 2 * group, hbm.at[n - 1, 0:HALO], hbm.at[n - 1, rows - HALO : rows], ref.at[n, top], ref.at[n, bot]).start()
+
+    Edge(SPACE, 0, cond_hbm.at[0:HALO], cond_hbm.at[rows - HALO : rows], c.at[top], c.at[bot]).start()
+    halo(0, steps, guess_hbm, g)
+    for i in range(steps - 1):
+        n = steps - i
+        halo((i + 1) // 2, n - 1, guess_hbm, g)
+        halo((i + 1) // 2, n, src_hbm, s)
+    halo(half - 1, 1, src_hbm, s)
     for load in loads:
         load.wait()
 
@@ -244,7 +243,7 @@
     a_e2 = Along(T_E2, c2.at[half, mid], c2.at[0, mid])
     a_u3 = Along(T_U3, u3.at[steps, mid], fu)
 
-    x_cond.wait_recv()
+    tiles(EARLY, 0, 4).wait_recv()
     for j in range(chunks):
         cc = c[:, at(j)]
         dd = 1.0 / (1.0 + 4.0 * cc)
@@ -252,12 +251,18 @@
         d[:, at(j)], w[:, at(j)] = dd, cc * dd
         dk[:, at(j)], wk[:, at(j)] = dd2, 2.0 * cc * dd2
     a_q.start()
-    guess_halo(steps).wait_recv()
 
     def local_step(i):
         n = steps - i
-        guess_halo(n - 1).wait_recv()
-        source_halo(n).wait_recv()
+        odd = lax.rem(i, 2) == 1
+
+        @pl.when(jnp.logical_and(odd, i < steps - 3))
+        def _():
+            tiles(EARLY, i + 1, 4).wait_recv()
+
+        @pl.when(i == steps - 3)
+        def _():
+            tiles(EARLY, i + 1, 5).wait_recv()
 
         @pl.when(i == 3)
         def _():
@@ -278,19 +283,18 @@
         start_g.wait()
         start_u.wait()
     a_guess.wait_recv()
-    f_guess = within(F_GUESS, g, slice(0, 1))
+    f_guess = within(0, g, slice(0, 1))
     f_guess.start()
     sweep_one(3, half + 1)
     each(4, half + 1, lambda m: coarse_defect(c1, m))
     a_e1.start()
     each(4, half + 1, lambda m: second_sweep(c1, ec, m, c2, wk, damping, inner=True))
     f_guess.wait_recv()
-    source_halo(1).wait_recv()
     each(1, 2, lambda n: first_sweep(g, n))
     a_e2.start()
     each(1, 2, lambda n: second_sweep(g, e, n, u1, w, damping))
     a_q.wait_recv()
-    f_q = within(F_Q, s, slice(0, 1))
+    f_q = within(1, s, slice(0, 1))
     f_q.start()
     f_q.wait_recv()
     each(0, 1, lambda n: first_sweep(g, n, has_prev=False))
@@ -300,10 +304,10 @@
     each(1, 2, lambda m: second_sweep(None, er, m, c0, wk, damping))
     sweep_one(2, 3)
     sweep_two(3, 4)
-    x_late = within(X_LATE, c2, slice(3, half + 1))
+    x_late = within(0, c2, slice(3, half + 1))
     x_late.start()
     a_e0.wait_recv()
-    f_e0 = within(F_E0, c0, slice(0, 1))
+    f_e0 = within(2, c0, slice(0, 1))
     f_e0.start()
     x_late.wait_recv()
     each(half, half + 1, prolong)
@@ -315,7 +319,7 @@
     a_u3.start()
     each(1, 2, lambda m: second_sweep(c0, ec, m, c1, wk, damping))
     sweep_two(2, 3)
-    x_mid = within(X_MID, c2, slice(2, 3))
+    x_mid = within(1, c2, slice(2, 3))
     x_mid.start()
     for j in range(chunks):
         u2[steps - 2, :, at(j)] = u1[steps - 2, :, at(j)] + c2[half - 1, :, at(j)]
@@ -323,7 +327,7 @@
     each(steps - 1, steps, lambda n: second_sweep(u2, e, n, u3, w, damping))
     each(steps, steps + 1, last_residual)
     a_e1.wait_recv()
-    f_e1 = within(F_E1, c1, slice(0, 1))
+    f_e1 = within(3, c1, slice(0, 1))
     f_e1.start()
     x_mid.wait_recv()
     each(3, half, prolong)
@@ -333,11 +337,11 @@
     each(5, steps - 1, lambda n: second_sweep(u2, e, n, u3, w, damping))
     f_e1.wait_recv()
     sweep_two(1, 2)
-    x_early = within(X_EARLY, c2, slice(1, 2))
+    x_early = within(0, c2, slice(1, 2))
     x_early.start()
     each(6, steps, last_residual)
     a_e2.wait_recv()
-    f_e2 = within(F_E2, c2, slice(0, 1))
+    f_e2 = within(2, c2, slice(0, 1))
     f_e2.start()
     x_early.wait_recv()
     for j in range(chunks):
@@ -354,8 +358,9 @@
     each(1, 3, lambda n: second_sweep(u2, e, n, u3, w, damping))
     each(2, 4, last_residual)
     each(1, 2, lambda n: last_residual(n, has_prev=False))
-    for copy in sent:
-        copy.wait_send()
+    tiles(EARLY, 0, 2 * steps).wait_send()
+    tiles(SPACE, 0, half + 6).wait_send()
+    Along(T_U3, s.at[0:PLANES, mid], s.at[0:PLANES, mid]).wait_send()
     a_u3.wait_recv()
     rbuf[0] = rbuf[0] + fu[...]
 
@@ -393,9 +398,9 @@
                 buf(half + 1), buf(half + 1), buf(half + 1), buf(steps + 1),
                 pltpu.VMEM((rows, cols), jnp.float32),
                 pltpu.VMEM((rows, cols), jnp.float32),
-                pltpu.SemaphoreType.DMA((STEPS + 4 * steps,)),
-                pltpu.SemaphoreType.DMA((STEPS + 4 * steps,)),
                 pltpu.SemaphoreType.DMA((5,)),
+                pltpu.SemaphoreType.DMA((steps + 2 * SETS + PLANES,)),
+                pltpu.SemaphoreType.DMA((6,)),
             ],
             compiler_params=pltpu.CompilerParams(
                 collective_id=0, has_side_effects=True, vmem_limit_bytes=59 * 1024 * 1024),

time: 42.3 us -> 41.2 us (0.974)
  Pallas kernels: 41.5 us -> 40.5 us
    pallas_call x1, Pallas kernels: 39.5 us -> 38.4 us  [shards(): pl.pallas_call(functools.partial(kernel, tms, spaces), out_shape=(buf(ste...]
where the time goes in v2:
time: 41.2 us; the launch traced here: 41.1 us
  Pallas kernels  40.5 us (98%)
  between operations  0.64 us (2%)
    pallas_call x1, Pallas kernels, shards(): pl.pallas_call(functools.partial(kernel, tms, spaces), out_shape=(buf(ste...  38.4 us
    pallas_call x1, Pallas kernels, shards(): pl.pallas_call(store, out_shape=(jax.ShapeDtypeStruct(source.shape, jnp.f...  2.03 us

profile of v2, /device:TPU:5, one launch (start us, length us, event | category | flops | bytes accessed | tf_op | source)
XLA Modules:
  0.0 41.1 jit_solution(9899703042668430869)
XLA Ops:
  0.6 38.4 %shard_map.59 = (f32[9,80,1024]{2,1,0:T(8,128)S(1)}, f32[8,64,1024]{2,1,0:T(8,128)S(1)}) custom-call(f32[8,64,1024]{2,1,0:T(8,128)} %src_hbm.1, f32[8,64,1024]{2,1,0:T(8,128)} %guess_hbm.1, f32[64,1024]{1,0:T(8,128)} %start_hbm.1, f32[64,1024]{1,0:T(8,128)} %cond_hbm.1), custom_call_target="tpu_custom_call" | custom-call | tf_op jit(solution)/shard_map/pallas_call | solution.py:390
  39.1 2.0 %shard_map.60 = (f32[8,64,1024]{2,1,0:T(8,128)}, f32[8,64,1024]{2,1,0:T(8,128)}) custom-call(f32[9,80,1024]{2,1,0:T(8,128)S(1)} %get-tuple-element.4.u3, f32[8,64,1024]{2,1,0:T(8,128)S(1)} %get-tuple-element.5.rbuf), custom_call_target="tpu_custom_call" | custom-call | tf_op jit(solution)/shard_map/pallas_call | solution.py:408

commit v3 on v2

--- a/solution.py
+++ b/solution.py
@@ -13,8 +13,8 @@
 LANES = 128
 
 EARLY, SPACE, ALONG = range(0, 6, 2)
-T_GUESS, T_Q, T_E0, T_E1, T_E2, T_U3 = range(6)
-SETS, PLANES = 4, 6
+T_GUESS, T_Q, T_E0, T_E1_RIM, T_E1, T_E2_RIM, T_E2, T_U3 = range(8)
+SETS, PLANES, PARTS = 4, 6, 8
 
 
 def kernel(
@@ -94,6 +94,18 @@
             def _():
                 remote(self.src, self.dst, ALONG, self.k, {"tm": t + 1}).wait_send()
 
+    class Split:
+        def __init__(self, k, ref):
+            def part(k, rows_of):
+                return Along(k, ref.at[half, rows_of], ref.at[0, rows_of])
+            self.rim = Along(k, s.at[0, 0 : 2 * HALO], s.at[0, 0 : 2 * HALO])
+            self.rest = part(k + 1, slice(2 * HALO, rows))
+            self.parts = [part(k, top_in), part(k, bot_in), self.rest]
+
+        def start(self):
+            for part in self.parts:
+                part.start()
+
     def within(turn, ref, sl):
         return Edge(SPACE, first_set + 2 * turn, ref.at[sl, top_in], ref.at[sl, bot_in], ref.at[sl, top], ref.at[sl, bot])
 
@@ -239,8 +251,8 @@
         qbuf[:, at(j)] = s[steps, mid, at(j)] + g[steps - 1, mid, at(j)]
     a_q = Along(T_Q, qbuf, s.at[0, mid])
     a_e0 = Along(T_E0, c0.at[half, mid], c0.at[0, mid])
-    a_e1 = Along(T_E1, c1.at[half, mid], c1.at[0, mid])
-    a_e2 = Along(T_E2, c2.at[half, mid], c2.at[0, mid])
+    a_e1 = Split(T_E1_RIM, c1)
+    a_e2 = Split(T_E2_RIM, c2)
     a_u3 = Along(T_U3, u3.at[steps, mid], fu)
 
     tiles(EARLY, 0, 4).wait_recv()
@@ -314,6 +326,9 @@
     each(steps, steps + 1, lambda n: first_sweep(u2, n))
     each(steps, steps + 1, lambda n: second_sweep(u2, e, n, u3, w, damping))
 
+    a_e1.rim.wait_recv()
+    f_e1 = within(3, c1, slice(0, 1))
+    f_e1.start()
     f_e0.wait_recv()
     each(1, 2, lambda m: coarse_defect(c0, m))
     a_u3.start()
@@ -326,23 +341,21 @@
     each(steps - 1, steps, lambda n: first_sweep(u2, n))
     each(steps - 1, steps, lambda n: second_sweep(u2, e, n, u3, w, damping))
     each(steps, steps + 1, last_residual)
-    a_e1.wait_recv()
-    f_e1 = within(3, c1, slice(0, 1))
-    f_e1.start()
-    x_mid.wait_recv()
-    each(3, half, prolong)
-    for j in range(chunks):
-        u2[4, :, at(j)] = u1[4, :, at(j)] + c2[2, :, at(j)]
-    each(5, steps - 1, lambda n: first_sweep(u2, n))
-    each(5, steps - 1, lambda n: second_sweep(u2, e, n, u3, w, damping))
+    a_e1.rest.wait_recv()
     f_e1.wait_recv()
     sweep_two(1, 2)
     x_early = within(0, c2, slice(1, 2))
     x_early.start()
-    each(6, steps, last_residual)
-    a_e2.wait_recv()
+    x_mid.wait_recv()
+    each(3, half, prolong)
+    for j in range(chunks):
+        u2[4, :, at(j)] = u1[4, :, at(j)] + c2[2, :, at(j)]
+    each(5, steps - 1, lambda n: first_sweep(u2, n))
+    each(5, steps - 1, lambda n: second_sweep(u2, e, n, u3, w, damping))
+    a_e2.rim.wait_recv()
     f_e2 = within(2, c2, slice(0, 1))
     f_e2.start()
+    each(6, steps, last_residual)
     x_early.wait_recv()
     for j in range(chunks):
         u2[2, :, at(j)] = u1[2, :, at(j)] + c2[1, :, at(j)]
@@ -350,6 +363,7 @@
     each(3, 5, lambda n: first_sweep(u2, n))
     each(3, 5, lambda n: second_sweep(u2, e, n, u3, w, damping))
     each(4, 6, last_residual)
+    a_e2.rest.wait_recv()
     f_e2.wait_recv()
     for j in range(chunks):
         u2[0, :, at(j)] = u1[0, :, at(j)] + c2[0, :, at(j)]
@@ -399,7 +413,7 @@
                 pltpu.VMEM((rows, cols), jnp.float32),
                 pltpu.VMEM((rows, cols), jnp.float32),
                 pltpu.SemaphoreType.DMA((5,)),
-                pltpu.SemaphoreType.DMA((steps + 2 * SETS + PLANES,)),
+                pltpu.SemaphoreType.DMA((steps + 2 * SETS + PARTS,)),
                 pltpu.SemaphoreType.DMA((6,)),
             ],
             compiler_params=pltpu.CompilerParams(

time: 41.2 us -> 40.9 us (level)
  the two profiles are of different devices: /device:TPU:5 before, /device:TPU:0 now
where the time goes in v3:
time: 40.9 us; the launch traced here: 40.3 us
  Pallas kernels  39.7 us (97%)
  between operations  0.64 us (2%)
    pallas_call x1, Pallas kernels, shards(): pl.pallas_call(functools.partial(kernel, tms, spaces), out_shape=(buf(ste...  37.6 us
    pallas_call x1, Pallas kernels, shards(): pl.pallas_call(store, out_shape=(jax.ShapeDtypeStruct(source.shape, jnp.f...  2.03 us

profile of v3, /device:TPU:0, one launch (start us, length us, event | category | flops | bytes accessed | tf_op | source)
XLA Modules:
  0.0 40.3 jit_solution(10543298605981187220)
XLA Ops:
  0.6 37.6 %shard_map.59 = (f32[9,80,1024]{2,1,0:T(8,128)S(1)}, f32[8,64,1024]{2,1,0:T(8,128)S(1)}) custom-call(f32[8,64,1024]{2,1,0:T(8,128)} %src_hbm.1, f32[8,64,1024]{2,1,0:T(8,128)} %guess_hbm.1, f32[64,1024]{1,0:T(8,128)} %start_hbm.1, f32[64,1024]{1,0:T(8,128)} %cond_hbm.1), custom_call_target="tpu_custom_call" | custom-call | tf_op jit(solution)/shard_map/pallas_call | solution.py:404
  38.3 2.0 %shard_map.60 = (f32[8,64,1024]{2,1,0:T(8,128)}, f32[8,64,1024]{2,1,0:T(8,128)}) custom-call(f32[9,80,1024]{2,1,0:T(8,128)S(1)} %get-tuple-element.4.u3, f32[8,64,1024]{2,1,0:T(8,128)S(1)} %get-tuple-element.5.rbuf), custom_call_target="tpu_custom_call" | custom-call | tf_op jit(solution)/shard_map/pallas_call | solution.py:422

commit v4 on v3

--- a/solution.py
+++ b/solution.py
@@ -12,20 +12,23 @@
 HALO = 8
 LANES = 128
 
-EARLY, SPACE, ALONG = range(0, 6, 2)
-T_GUESS, T_Q, T_E0, T_E1_RIM, T_E1, T_E2_RIM, T_E2, T_U3 = range(8)
-SETS, PLANES, PARTS = 4, 6, 8
+EARLY, SPACE, ALONG, RELAY = 0, 2, 4, 5
+T_GUESS, T_Q, T_E0, T_E1_RIM, T_E1, T_E2_RIM, T_E2, T_U3, T_RELAY = range(9)
+SETS, PLANES, PARTS = 4, 6, 9
+RELAYED = 2 * HALO
 
 
 def kernel(
     tms, spaces, src_hbm, guess_hbm, start_hbm, cond_hbm, u3, rbuf,
     g, s, c, d, w, dk, wk, e, u1, er, ec, c0, c1, c2, u2, qbuf, fu,
-    send_sem, recv_sem, load_sem,
+    relay, send_sem, recv_sem,
 ):
     t = lax.axis_index("tm")
     z = lax.axis_index("space")
     has_up, has_dn = z > 0, z < spaces - 1
     has_before, has_after = t > 0, t < tms - 1
+    by_relay = jnp.logical_and(lax.rem(t, 2) == 1, t + 2 < tms)
+    is_relay = jnp.logical_and(lax.rem(t, 2) == 1, t > 2)
     steps, rows, cols = src_hbm.shape
     half = steps // 2
     full = rows + 2 * HALO
@@ -114,22 +117,25 @@
         return Edge(sent, k, ref, ref, ref, ref)
 
     barrier = pltpu.get_barrier_semaphore()
-    for flag, dev in ((has_up, up), (has_dn, dn), (has_before, {"tm": t - 1}), (has_after, {"tm": t + 1})):
+    peers = (
+        (has_up, up), (has_dn, dn), (has_before, {"tm": t - 1}), (has_after, {"tm": t + 1}),
+        (is_relay, {"tm": t - 2}), (by_relay, {"tm": t + 2}))
+    for flag, dev in peers:
         @pl.when(flag)
         def _(dev=dev):
             pl.semaphore_signal(barrier, inc=1, device_id=dev, device_id_type=MESH)
 
-    last_guess = pltpu.make_async_copy(guess_hbm.at[steps - 1], g.at[steps, mid], load_sem.at[0])
+    last_guess = pltpu.make_async_copy(guess_hbm.at[steps - 1], g.at[steps, mid], send_sem.at[ALONG])
     last_guess.start()
     loads = [
-        pltpu.make_async_copy(cond_hbm, c.at[mid], load_sem.at[1]),
-        pltpu.make_async_copy(src_hbm, s.at[later, mid], load_sem.at[2]),
-        pltpu.make_async_copy(guess_hbm.at[0 : steps - 1], g.at[1:steps, mid], load_sem.at[3]),
+        pltpu.make_async_copy(cond_hbm, c.at[mid], recv_sem.at[first_plane - 1]),
+        pltpu.make_async_copy(src_hbm, s.at[later, mid], recv_sem.at[first_plane - 2]),
+        pltpu.make_async_copy(guess_hbm.at[0 : steps - 1], g.at[1:steps, mid], recv_sem.at[first_plane - 3]),
     ]
     for load in loads:
         load.start()
-    start_g = pltpu.make_async_copy(start_hbm, g.at[0, mid], load_sem.at[4])
-    start_u = pltpu.make_async_copy(start_hbm, fu, load_sem.at[5])
+    start_g = pltpu.make_async_copy(start_hbm, g.at[0, mid], recv_sem.at[first_plane + T_GUESS])
+    start_u = pltpu.make_async_copy(start_hbm, fu, recv_sem.at[first_plane + T_U3])
 
     @pl.when(jnp.logical_not(has_before))
     def _():
@@ -149,8 +155,7 @@
                 else:
                     ref[0, edge] = jnp.zeros((HALO, cols), jnp.float32)
 
-    peers = sum(jnp.where(flag, 1, 0) for flag in (has_up, has_dn, has_before, has_after))
-    pl.semaphore_wait(barrier, peers)
+    pl.semaphore_wait(barrier, sum(jnp.where(flag, 1, 0) for flag, _ in peers))
 
     a_guess = Along(T_GUESS, g.at[steps, mid], g.at[0, mid])
     last_guess.wait()
@@ -253,7 +258,30 @@
     a_e0 = Along(T_E0, c0.at[half, mid], c0.at[0, mid])
     a_e1 = Split(T_E1_RIM, c1)
     a_e2 = Split(T_E2_RIM, c2)
-    a_u3 = Along(T_U3, u3.at[steps, mid], fu)
+    a_u3 = Along(T_U3, fu, fu)
+    kept = rows - RELAYED
+    u3_kept = Along(T_U3, u3.at[steps, HALO : HALO + kept], fu.at[0:kept])
+    u3_rest = Along(T_U3, u3.at[steps, HALO + kept : HALO + rows], fu.at[kept:rows])
+
+    def to_relay(sent, k, src, dst, step):
+        return remote(src, dst, sent, first_plane + k, {"tm": t + step})
+
+    def start_u3():
+        u3_kept.start()
+
+        @pl.when(jnp.logical_not(by_relay))
+        def _():
+            u3_rest.start()
+
+        @pl.when(by_relay)
+        def _():
+            to_relay(ALONG, T_RELAY, u3_rest.src, relay, 2).start()
+
+    def pass_on():
+        @pl.when(is_relay)
+        def _():
+            to_relay(RELAY, T_RELAY, relay, relay, -2).wait_recv()
+            to_relay(RELAY, T_U3, relay, u3_rest.dst, -1).start()
 
     tiles(EARLY, 0, 4).wait_recv()
     for j in range(chunks):
@@ -331,7 +359,7 @@
     f_e1.start()
     f_e0.wait_recv()
     each(1, 2, lambda m: coarse_defect(c0, m))
-    a_u3.start()
+    start_u3()
     each(1, 2, lambda m: second_sweep(c0, ec, m, c1, wk, damping))
     sweep_two(2, 3)
     x_mid = within(1, c2, slice(2, 3))
@@ -352,6 +380,7 @@
         u2[4, :, at(j)] = u1[4, :, at(j)] + c2[2, :, at(j)]
     each(5, steps - 1, lambda n: first_sweep(u2, n))
     each(5, steps - 1, lambda n: second_sweep(u2, e, n, u3, w, damping))
+    pass_on()
     a_e2.rim.wait_recv()
     f_e2 = within(2, c2, slice(0, 1))
     f_e2.start()
@@ -375,6 +404,10 @@
     tiles(EARLY, 0, 2 * steps).wait_send()
     tiles(SPACE, 0, half + 6).wait_send()
     Along(T_U3, s.at[0:PLANES, mid], s.at[0:PLANES, mid]).wait_send()
+
+    @pl.when(is_relay)
+    def _():
+        to_relay(RELAY, T_U3, relay, u3_rest.dst, -1).wait_send()
     a_u3.wait_recv()
     rbuf[0] = rbuf[0] + fu[...]
 
@@ -412,9 +445,9 @@
                 buf(half + 1), buf(half + 1), buf(half + 1), buf(steps + 1),
                 pltpu.VMEM((rows, cols), jnp.float32),
                 pltpu.VMEM((rows, cols), jnp.float32),
-                pltpu.SemaphoreType.DMA((5,)),
+                pltpu.VMEM((RELAYED, cols), jnp.float32),
+                pltpu.SemaphoreType.DMA((6,)),
                 pltpu.SemaphoreType.DMA((steps + 2 * SETS + PARTS,)),
-                pltpu.SemaphoreType.DMA((6,)),
             ],
             compiler_params=pltpu.CompilerParams(
                 collective_id=0, has_side_effects=True, vmem_limit_bytes=59 * 1024 * 1024),

time: 40.9 us -> 40.4 us (0.988); the launches traced: 40.3 us -> 40.3 us
  no operation moved by 1% of the time
where the time goes in v4:
time: 40.4 us; the launch traced here: 40.3 us
  Pallas kernels  39.6 us (98%)
  between operations  0.64 us (2%)
    pallas_call x1, Pallas kernels, shards(): pl.pallas_call(functools.partial(kernel, tms, spaces), out_shape=(buf(ste...  37.6 us
    pallas_call x1, Pallas kernels, shards(): pl.pallas_call(store, out_shape=(jax.ShapeDtypeStruct(source.shape, jnp.f...  2.03 us

profile of v4, /device:TPU:0, one launch (start us, length us, event | category | flops | bytes accessed | tf_op | source)
XLA Modules:
  0.0 40.3 jit_solution(1581373239304638467)
XLA Ops:
  0.6 37.6 %shard_map.59 = (f32[9,80,1024]{2,1,0:T(8,128)S(1)}, f32[8,64,1024]{2,1,0:T(8,128)S(1)}) custom-call(f32[8,64,1024]{2,1,0:T(8,128)} %src_hbm.1, f32[8,64,1024]{2,1,0:T(8,128)} %guess_hbm.1, f32[64,1024]{1,0:T(8,128)} %start_hbm.1, f32[64,1024]{1,0:T(8,128)} %cond_hbm.1), custom_call_target="tpu_custom_call" | custom-call | tf_op jit(solution)/shard_map/pallas_call | solution.py:437
  38.2 2.0 %shard_map.60 = (f32[8,64,1024]{2,1,0:T(8,128)}, f32[8,64,1024]{2,1,0:T(8,128)}) custom-call(f32[9,80,1024]{2,1,0:T(8,128)S(1)} %get-tuple-element.4.u3, f32[8,64,1024]{2,1,0:T(8,128)S(1)} %get-tuple-element.5.rbuf), custom_call_target="tpu_custom_call" | custom-call | tf_op jit(solution)/shard_map/pallas_call | solution.py:455

commit v5 on v4

--- a/solution.py
+++ b/solution.py
@@ -21,7 +21,7 @@
 def kernel(
     tms, spaces, src_hbm, guess_hbm, start_hbm, cond_hbm, u3, rbuf,
     g, s, c, d, w, dk, wk, e, u1, er, ec, c0, c1, c2, u2, qbuf, fu,
-    relay, send_sem, recv_sem,
+    relay, send_sem, recv_sem, ready,
 ):
     t = lax.axis_index("tm")
     z = lax.axis_index("space")
@@ -29,6 +29,12 @@
     has_before, has_after = t > 0, t < tms - 1
     by_relay = jnp.logical_and(lax.rem(t, 2) == 1, t + 2 < tms)
     is_relay = jnp.logical_and(lax.rem(t, 2) == 1, t > 2)
+    from_relay = jnp.logical_and(lax.rem(t, 2) == 0, jnp.logical_and(t > 0, t + 1 < tms))
+    odd_row = lax.rem(z, 2) == 1
+    even_row = jnp.logical_not(odd_row)
+
+    def count(*flags):
+        return sum(jnp.where(flag, 1, 0) for flag in flags)
     steps, rows, cols = src_hbm.shape
     half = steps // 2
     full = rows + 2 * HALO
@@ -117,10 +123,10 @@
         return Edge(sent, k, ref, ref, ref, ref)
 
     barrier = pltpu.get_barrier_semaphore()
-    peers = (
-        (has_up, up), (has_dn, dn), (has_before, {"tm": t - 1}), (has_after, {"tm": t + 1}),
-        (is_relay, {"tm": t - 2}), (by_relay, {"tm": t + 2}))
-    for flag, dev in peers:
+    greeted = (
+        (has_before, {"tm": t - 1}), (is_relay, {"tm": t - 2}), (from_relay, {"tm": t + 1}),
+        (jnp.logical_and(odd_row, has_up), up), (jnp.logical_and(odd_row, has_dn), dn))
+    for flag, dev in greeted:
         @pl.when(flag)
         def _(dev=dev):
             pl.semaphore_signal(barrier, inc=1, device_id=dev, device_id_type=MESH)
@@ -155,11 +161,24 @@
                 else:
                     ref[0, edge] = jnp.zeros((HALO, cols), jnp.float32)
 
-    pl.semaphore_wait(barrier, sum(jnp.where(flag, 1, 0) for flag, _ in peers))
+    rows_beside = count(has_up, has_dn)
+    greetings = count(has_after, by_relay, is_relay) + jnp.where(even_row, rows_beside, 0)
+
+    @pl.when(greetings > 0)
+    def _():
+        pl.semaphore_wait(barrier, greetings)
+    for flag, dev in ((has_up, up), (has_dn, dn)):
+        @pl.when(jnp.logical_and(even_row, flag))
+        def _(dev=dev):
+            pl.semaphore_signal(ready, inc=1, device_id=dev, device_id_type=MESH)
 
     a_guess = Along(T_GUESS, g.at[steps, mid], g.at[0, mid])
     last_guess.wait()
     a_guess.start()
+
+    @pl.when(jnp.logical_and(odd_row, rows_beside > 0))
+    def _():
+        pl.semaphore_wait(ready, rows_beside)
 
     def halo(group, n, hbm, ref):
         Edge(EARLY, 2 * group, hbm.at[n - 1, 0:HALO], hbm.at[n - 1, rows - HALO : rows], ref.at[n, top], ref.at[n, bot]).start()
@@ -283,14 +302,19 @@
             to_relay(RELAY, T_RELAY, relay, relay, -2).wait_recv()
             to_relay(RELAY, T_U3, relay, u3_rest.dst, -1).start()
 
+    def coefficients(part):
+        for j in range(chunks):
+            cc = c[part, at(j)]
+            dd = 1.0 / (1.0 + 4.0 * cc)
+            dd2 = 1.0 / (1.0 + 8.0 * cc)
+            d[part, at(j)], w[part, at(j)] = dd, cc * dd
+            dk[part, at(j)], wk[part, at(j)] = dd2, 2.0 * cc * dd2
+
+    coefficients(mid)
+    a_q.start()
     tiles(EARLY, 0, 4).wait_recv()
-    for j in range(chunks):
-        cc = c[:, at(j)]
-        dd = 1.0 / (1.0 + 4.0 * cc)
-        dd2 = 1.0 / (1.0 + 8.0 * cc)
-        d[:, at(j)], w[:, at(j)] = dd, cc * dd
-        dk[:, at(j)], wk[:, at(j)] = dd2, 2.0 * cc * dd2
-    a_q.start()
+    coefficients(top)
+    coefficients(bot)
 
     def local_step(i):
         n = steps - i
@@ -448,6 +472,7 @@
                 pltpu.VMEM((RELAYED, cols), jnp.float32),
                 pltpu.SemaphoreType.DMA((6,)),
                 pltpu.SemaphoreType.DMA((steps + 2 * SETS + PARTS,)),
+                pltpu.SemaphoreType.REGULAR,
             ],
             compiler_params=pltpu.CompilerParams(
                 collective_id=0, has_side_effects=True, vmem_limit_bytes=59 * 1024 * 1024),

time: 40.4 us -> 39.8 us (0.985)
  Pallas kernels: 39.6 us -> 39 us
    pallas_call x1, Pallas kernels: 37.6 us -> 37 us  [shards(): pl.pallas_call(functools.partial(kernel, tms, spaces), out_shape=(buf(ste...]
where the time goes in v5:
time: 39.8 us; the launch traced here: 39.6 us
  Pallas kernels  39 us (98%)
  between operations  0.64 us (2%)
    pallas_call x1, Pallas kernels, shards(): pl.pallas_call(functools.partial(kernel, tms, spaces), out_shape=(buf(ste...  37 us
    pallas_call x1, Pallas kernels, shards(): pl.pallas_call(store, out_shape=(jax.ShapeDtypeStruct(source.shape, jnp.f...  2.03 us

profile of v5, /device:TPU:0, one launch (start us, length us, event | category | flops | bytes accessed | tf_op | source)
XLA Modules:
  0.0 39.6 jit_solution(3039124452580615489)
XLA Ops:
  0.6 37.0 %shard_map.59 = (f32[9,80,1024]{2,1,0:T(8,128)S(1)}, f32[8,64,1024]{2,1,0:T(8,128)S(1)}) custom-call(f32[8,64,1024]{2,1,0:T(8,128)} %src_hbm.1, f32[8,64,1024]{2,1,0:T(8,128)} %guess_hbm.1, f32[64,1024]{1,0:T(8,128)} %start_hbm.1, f32[64,1024]{1,0:T(8,128)} %cond_hbm.1), custom_call_target="tpu_custom_call" | custom-call | tf_op jit(solution)/shard_map/pallas_call | solution.py:461
  37.6 2.0 %shard_map.60 = (f32[8,64,1024]{2,1,0:T(8,128)}, f32[8,64,1024]{2,1,0:T(8,128)}) custom-call(f32[9,80,1024]{2,1,0:T(8,128)S(1)} %get-tuple-element.4.u3, f32[8,64,1024]{2,1,0:T(8,128)S(1)} %get-tuple-element.5.rbuf), custom_call_target="tpu_custom_call" | custom-call | tf_op jit(solution)/shard_map/pallas_call | solution.py:480

commit v6 on v5

--- a/solution.py
+++ b/solution.py
@@ -12,7 +12,7 @@
 HALO = 8
 LANES = 128
 
-EARLY, SPACE, ALONG, RELAY = 0, 2, 4, 5
+EARLY, SPACE, ALONG, RELAY = range(4)
 T_GUESS, T_Q, T_E0, T_E1_RIM, T_E1, T_E2_RIM, T_E2, T_U3, T_RELAY = range(9)
 SETS, PLANES, PARTS = 4, 6, 9
 RELAYED = 2 * HALO
@@ -50,12 +50,33 @@
             device_id=dev, device_id_type=MESH)
 
     up, dn = {"space": z - 1}, {"space": z + 1}
-    first_set = 2 * half
-    first_plane = first_set + 2 * SETS
-
-    class Edge:
-        def __init__(self, sent, k, first, last, halo_top, halo_bot):
-            self.sent, self.k, self.first, self.last, self.top, self.bot = sent, k, first, last, halo_top, halo_bot
+    first_set = half
+    first_plane = first_set + SETS
+    rows_beside = count(has_up, has_dn)
+    beside = {"space": jnp.where(has_up, z - 1, z + 1)}
+
+    class Tiles:
+        def __init__(self, sent, k, n):
+            self.sent, self.k, self.n = sent, k, n
+
+        def each_count(self, wait):
+            for beside_count in (1, 2):
+                @pl.when(rows_beside == beside_count)
+                def _(n=self.n * beside_count):
+                    planes = next(p for p in range(1, steps + 1) if n % p == 0 and n // p * HALO <= full)
+                    ref = s.at[0:planes, 0 : n // planes * HALO]
+                    wait(remote(ref, ref, self.sent, self.k, beside))
+
+        def wait_recv(self):
+            self.each_count(lambda copy: copy.wait_recv())
+
+        def wait_send(self):
+            self.each_count(lambda copy: copy.wait_send())
+
+    class Edge(Tiles):
+        def __init__(self, sent, k, first, last, halo_top, halo_bot, n=1):
+            super().__init__(sent, k, n)
+            self.first, self.last, self.top, self.bot = first, last, halo_top, halo_bot
 
         def start(self):
             @pl.when(has_up)
@@ -64,25 +85,7 @@
 
             @pl.when(has_dn)
             def _():
-                remote(self.last, self.top, self.sent + 1, self.k + 1, dn).start()
-
-        def wait_recv(self):
-            @pl.when(has_dn)
-            def _():
-                remote(self.first, self.bot, self.sent, self.k, dn).wait_recv()
-
-            @pl.when(has_up)
-            def _():
-                remote(self.last, self.top, self.sent + 1, self.k + 1, up).wait_recv()
-
-        def wait_send(self):
-            @pl.when(has_up)
-            def _():
-                remote(self.first, self.bot, self.sent, self.k, up).wait_send()
-
-            @pl.when(has_dn)
-            def _():
-                remote(self.last, self.top, self.sent + 1, self.k + 1, dn).wait_send()
+                remote(self.last, self.top, self.sent, self.k, dn).start()
 
     class Along:
         def __init__(self, k, src, dst):
@@ -116,11 +119,9 @@
                 part.start()
 
     def within(turn, ref, sl):
-        return Edge(SPACE, first_set + 2 * turn, ref.at[sl, top_in], ref.at[sl, bot_in], ref.at[sl, top], ref.at[sl, bot])
-
-    def tiles(sent, k, count):
-        ref = s.at[0:1, 0 : count * HALO] if count * HALO <= full else s.at[0:2, 0 : count * HALO // 2]
-        return Edge(sent, k, ref, ref, ref, ref)
+        return Edge(
+            SPACE, first_set + turn, ref.at[sl, top_in], ref.at[sl, bot_in], ref.at[sl, top], ref.at[sl, bot],
+            sl.stop - sl.start)
 
     barrier = pltpu.get_barrier_semaphore()
     greeted = (
@@ -161,7 +162,6 @@
                 else:
                     ref[0, edge] = jnp.zeros((HALO, cols), jnp.float32)
 
-    rows_beside = count(has_up, has_dn)
     greetings = count(has_after, by_relay, is_relay) + jnp.where(even_row, rows_beside, 0)
 
     @pl.when(greetings > 0)
@@ -181,7 +181,7 @@
         pl.semaphore_wait(ready, rows_beside)
 
     def halo(group, n, hbm, ref):
-        Edge(EARLY, 2 * group, hbm.at[n - 1, 0:HALO], hbm.at[n - 1, rows - HALO : rows], ref.at[n, top], ref.at[n, bot]).start()
+        Edge(EARLY, group, hbm.at[n - 1, 0:HALO], hbm.at[n - 1, rows - HALO : rows], ref.at[n, top], ref.at[n, bot]).start()
 
     Edge(SPACE, 0, cond_hbm.at[0:HALO], cond_hbm.at[rows - HALO : rows], c.at[top], c.at[bot]).start()
     halo(0, steps, guess_hbm, g)
@@ -312,7 +312,7 @@
 
     coefficients(mid)
     a_q.start()
-    tiles(EARLY, 0, 4).wait_recv()
+    Tiles(EARLY, 0, 4).wait_recv()
     coefficients(top)
     coefficients(bot)
 
@@ -322,11 +322,11 @@
 
         @pl.when(jnp.logical_and(odd, i < steps - 3))
         def _():
-            tiles(EARLY, i + 1, 4).wait_recv()
+            Tiles(EARLY, (i + 1) // 2, 4).wait_recv()
 
         @pl.when(i == steps - 3)
         def _():
-            tiles(EARLY, i + 1, 5).wait_recv()
+            Tiles(EARLY, half - 1, 5).wait_recv()
 
         @pl.when(i == 3)
         def _():
@@ -425,15 +425,21 @@
     each(1, 3, lambda n: second_sweep(u2, e, n, u3, w, damping))
     each(2, 4, last_residual)
     each(1, 2, lambda n: last_residual(n, has_prev=False))
-    tiles(EARLY, 0, 2 * steps).wait_send()
-    tiles(SPACE, 0, half + 6).wait_send()
+    @pl.when(jnp.logical_not(has_before))
+    def _():
+        rbuf[0] = rbuf[0] + fu[...]
+    Tiles(EARLY, 0, 2 * steps).wait_send()
+    Tiles(SPACE, 0, half + 6).wait_send()
     Along(T_U3, s.at[0:PLANES, mid], s.at[0:PLANES, mid]).wait_send()
 
     @pl.when(is_relay)
     def _():
         to_relay(RELAY, T_U3, relay, u3_rest.dst, -1).wait_send()
-    a_u3.wait_recv()
-    rbuf[0] = rbuf[0] + fu[...]
+
+    @pl.when(has_before)
+    def _():
+        a_u3.wait_recv()
+        rbuf[0] = rbuf[0] + fu[...]
 
 
 def store(u3, rbuf, u_out, r_out, sem):
@@ -470,8 +476,8 @@
                 pltpu.VMEM((rows, cols), jnp.float32),
                 pltpu.VMEM((rows, cols), jnp.float32),
                 pltpu.VMEM((RELAYED, cols), jnp.float32),
-                pltpu.SemaphoreType.DMA((6,)),
-                pltpu.SemaphoreType.DMA((steps + 2 * SETS + PARTS,)),
+                pltpu.SemaphoreType.DMA((4,)),
+                pltpu.SemaphoreType.DMA((half + SETS + PARTS,)),
                 pltpu.SemaphoreType.REGULAR,
             ],
             compiler_params=pltpu.CompilerParams(

time: 39.8 us -> 39.7 us (level)
  no operation moved by 1% of the time
where the time goes in v6:
time: 39.7 us; the launch traced here: 39.5 us
  Pallas kernels  38.9 us (98%)
  between operations  0.64 us (2%)
    pallas_call x1, Pallas kernels, shards(): pl.pallas_call(functools.partial(kernel, tms, spaces), out_shape=(buf(ste...  36.9 us
    pallas_call x1, Pallas kernels, shards(): pl.pallas_call(store, out_shape=(jax.ShapeDtypeStruct(source.shape, jnp.f...  2.03 us

profile of v6, /device:TPU:0, one launch (start us, length us, event | category | flops | bytes accessed | tf_op | source)
XLA Modules:
  0.0 39.5 jit_solution(9982324037381891339)
XLA Ops:
  0.6 36.9 %shard_map.59 = (f32[9,80,1024]{2,1,0:T(8,128)S(1)}, f32[8,64,1024]{2,1,0:T(8,128)S(1)}) custom-call(f32[8,64,1024]{2,1,0:T(8,128)} %src_hbm.1, f32[8,64,1024]{2,1,0:T(8,128)} %guess_hbm.1, f32[64,1024]{1,0:T(8,128)} %start_hbm.1, f32[64,1024]{1,0:T(8,128)} %cond_hbm.1), custom_call_target="tpu_custom_call" | custom-call | tf_op jit(solution)/shard_map/pallas_call | solution.py:467
  37.5 2.0 %shard_map.60 = (f32[8,64,1024]{2,1,0:T(8,128)}, f32[8,64,1024]{2,1,0:T(8,128)}) custom-call(f32[9,80,1024]{2,1,0:T(8,128)S(1)} %get-tuple-element.4.u3, f32[8,64,1024]{2,1,0:T(8,128)S(1)} %get-tuple-element.5.rbuf), custom_call_target="tpu_custom_call" | custom-call | tf_op jit(solution)/shard_map/pallas_call | solution.py:486

commit v7 on v6

--- a/solution.py
+++ b/solution.py
@@ -15,7 +15,7 @@
 EARLY, SPACE, ALONG, RELAY = range(4)
 T_GUESS, T_Q, T_E0, T_E1_RIM, T_E1, T_E2_RIM, T_E2, T_U3, T_RELAY = range(9)
 SETS, PLANES, PARTS = 4, 6, 9
-RELAYED = 2 * HALO
+RELAYED = 3 * HALO
 
 
 def kernel(
@@ -32,6 +32,9 @@
     from_relay = jnp.logical_and(lax.rem(t, 2) == 0, jnp.logical_and(t > 0, t + 1 < tms))
     odd_row = lax.rem(z, 2) == 1
     even_row = jnp.logical_not(odd_row)
+    handing = jnp.logical_and(lax.rem(t, 2) == 0, has_after)
+    by_hand = jnp.logical_and(handing, jnp.logical_and(even_row, has_dn))
+    is_hand = jnp.logical_and(handing, odd_row)
 
     def count(*flags):
         return sum(jnp.where(flag, 1, 0) for flag in flags)
@@ -282,25 +285,37 @@
     u3_kept = Along(T_U3, u3.at[steps, HALO : HALO + kept], fu.at[0:kept])
     u3_rest = Along(T_U3, u3.at[steps, HALO + kept : HALO + rows], fu.at[kept:rows])
 
-    def to_relay(sent, k, src, dst, step):
-        return remote(src, dst, sent, first_plane + k, {"tm": t + step})
+    def give(sent, k, src, dst, step, row_step=0):
+        dev = {"tm": t + step, "space": z + row_step}
+        return remote(src, dst, sent, first_plane + k, dev)
 
     def start_u3():
         u3_kept.start()
 
-        @pl.when(jnp.logical_not(by_relay))
+        @pl.when(jnp.logical_not(jnp.logical_or(by_relay, by_hand)))
         def _():
             u3_rest.start()
 
         @pl.when(by_relay)
         def _():
-            to_relay(ALONG, T_RELAY, u3_rest.src, relay, 2).start()
-
-    def pass_on():
-        @pl.when(is_relay)
-        def _():
-            to_relay(RELAY, T_RELAY, relay, relay, -2).wait_recv()
-            to_relay(RELAY, T_U3, relay, u3_rest.dst, -1).start()
+            give(ALONG, T_RELAY, u3_rest.src, relay, 2).start()
+
+        @pl.when(by_hand)
+        def _():
+            give(ALONG, T_RELAY, u3_rest.src, relay, 0, 1).start()
+
+    def passed_on(act):
+        for flag, source, target in ((is_relay, (-2, 0), (-1, 0)), (is_hand, (0, -1), (1, -1))):
+            @pl.when(flag)
+            def _(source=source, target=target):
+                act(source, target)
+
+    def forward(source, target):
+        give(RELAY, T_RELAY, relay, relay, *source).wait_recv()
+        give(RELAY, T_U3, relay, u3_rest.dst, *target).start()
+
+    def forwarded(source, target):
+        give(RELAY, T_U3, relay, u3_rest.dst, *target).wait_send()
 
     def coefficients(part):
         for j in range(chunks):
@@ -404,7 +419,7 @@
         u2[4, :, at(j)] = u1[4, :, at(j)] + c2[2, :, at(j)]
     each(5, steps - 1, lambda n: first_sweep(u2, n))
     each(5, steps - 1, lambda n: second_sweep(u2, e, n, u3, w, damping))
-    pass_on()
+    passed_on(forward)
     a_e2.rim.wait_recv()
     f_e2 = within(2, c2, slice(0, 1))
     f_e2.start()
@@ -432,9 +447,7 @@
     Tiles(SPACE, 0, half + 6).wait_send()
     Along(T_U3, s.at[0:PLANES, mid], s.at[0:PLANES, mid]).wait_send()
 
-    @pl.when(is_relay)
-    def _():
-        to_relay(RELAY, T_U3, relay, u3_rest.dst, -1).wait_send()
+    passed_on(forwarded)
 
     @pl.when(has_before)
     def _():

time: 39.7 us -> 39.3 us (0.990); the launches traced: 39.5 us -> 38.6 us
  Pallas kernels: 38.9 us -> 37.9 us
    pallas_call x1, Pallas kernels: 36.9 us -> 35.9 us  [shards(): pl.pallas_call(functools.partial(kernel, tms, spaces), out_shape=(buf(ste...]
where the time goes in v7:
time: 39.3 us; the launch traced here: 38.6 us
  Pallas kernels  37.9 us (96%)
  between operations  0.64 us (2%)
    pallas_call x1, Pallas kernels, shards(): pl.pallas_call(functools.partial(kernel, tms, spaces), out_shape=(buf(ste...  35.9 us
    pallas_call x1, Pallas kernels, shards(): pl.pallas_call(store, out_shape=(jax.ShapeDtypeStruct(source.shape, jnp.f...  2.03 us

profile of v7, /device:TPU:0, one launch (start us, length us, event | category | flops | bytes accessed | tf_op | source)
XLA Modules:
  0.0 38.6 jit_solution(16710110976471701548)
XLA Ops:
  0.6 35.9 %shard_map.59 = (f32[9,80,1024]{2,1,0:T(8,128)S(1)}, f32[8,64,1024]{2,1,0:T(8,128)S(1)}) custom-call(f32[8,64,1024]{2,1,0:T(8,128)} %src_hbm.1, f32[8,64,1024]{2,1,0:T(8,128)} %guess_hbm.1, f32[64,1024]{1,0:T(8,128)} %start_hbm.1, f32[64,1024]{1,0:T(8,128)} %cond_hbm.1), custom_call_target="tpu_custom_call" | custom-call | tf_op jit(solution)/shard_map/pallas_call | solution.py:480
  36.5 2.0 %shard_map.60 = (f32[8,64,1024]{2,1,0:T(8,128)}, f32[8,64,1024]{2,1,0:T(8,128)}) custom-call(f32[9,80,1024]{2,1,0:T(8,128)S(1)} %get-tuple-element.4.u3, f32[8,64,1024]{2,1,0:T(8,128)S(1)} %get-tuple-element.5.rbuf), custom_call_target="tpu_custom_call" | custom-call | tf_op jit(solution)/shard_map/pallas_call | solution.py:499

commit v8 on v7

--- a/solution.py
+++ b/solution.py
@@ -14,7 +14,7 @@
 
 EARLY, SPACE, ALONG, RELAY = range(4)
 T_GUESS, T_Q, T_E0, T_E1_RIM, T_E1, T_E2_RIM, T_E2, T_U3, T_RELAY = range(9)
-SETS, PLANES, PARTS = 4, 6, 9
+PLANES, PARTS = 6, 9
 RELAYED = 3 * HALO
 
 
@@ -32,7 +32,8 @@
     from_relay = jnp.logical_and(lax.rem(t, 2) == 0, jnp.logical_and(t > 0, t + 1 < tms))
     odd_row = lax.rem(z, 2) == 1
     even_row = jnp.logical_not(odd_row)
-    handing = jnp.logical_and(lax.rem(t, 2) == 0, has_after)
+    paired = jnp.logical_or(lax.rem(z, 2) == 1, has_dn)
+    handing = jnp.logical_and(jnp.logical_and(lax.rem(t, 2) == 0, has_after), paired)
     by_hand = jnp.logical_and(handing, jnp.logical_and(even_row, has_dn))
     is_hand = jnp.logical_and(handing, odd_row)
 
@@ -53,8 +54,8 @@
             device_id=dev, device_id_type=MESH)
 
     up, dn = {"space": z - 1}, {"space": z + 1}
-    first_set = half
-    first_plane = first_set + SETS
+    alone = half
+    first_plane = half + 1
     rows_beside = count(has_up, has_dn)
     beside = {"space": jnp.where(has_up, z - 1, z + 1)}
 
@@ -123,7 +124,7 @@
 
     def within(turn, ref, sl):
         return Edge(
-            SPACE, first_set + turn, ref.at[sl, top_in], ref.at[sl, bot_in], ref.at[sl, top], ref.at[sl, bot],
+            SPACE, turn, ref.at[sl, top_in], ref.at[sl, bot_in], ref.at[sl, top], ref.at[sl, bot],
             sl.stop - sl.start)
 
     barrier = pltpu.get_barrier_semaphore()
@@ -138,12 +139,13 @@
     last_guess = pltpu.make_async_copy(guess_hbm.at[steps - 1], g.at[steps, mid], send_sem.at[ALONG])
     last_guess.start()
     loads = [
-        pltpu.make_async_copy(cond_hbm, c.at[mid], recv_sem.at[first_plane - 1]),
-        pltpu.make_async_copy(src_hbm, s.at[later, mid], recv_sem.at[first_plane - 2]),
-        pltpu.make_async_copy(guess_hbm.at[0 : steps - 1], g.at[1:steps, mid], recv_sem.at[first_plane - 3]),
+        pltpu.make_async_copy(cond_hbm, c.at[mid], recv_sem.at[alone]),
+        pltpu.make_async_copy(src_hbm, s.at[later, mid], send_sem.at[RELAY]),
+        pltpu.make_async_copy(guess_hbm.at[0 : steps - 1], g.at[1:steps, mid], recv_sem.at[alone]),
     ]
     for load in loads:
         load.start()
+    loaded = [loads[1], pltpu.make_async_copy(src_hbm, s.at[later, mid], recv_sem.at[alone])]
     start_g = pltpu.make_async_copy(start_hbm, g.at[0, mid], recv_sem.at[first_plane + T_GUESS])
     start_u = pltpu.make_async_copy(start_hbm, fu, recv_sem.at[first_plane + T_U3])
 
@@ -170,14 +172,14 @@
     @pl.when(greetings > 0)
     def _():
         pl.semaphore_wait(barrier, greetings)
+
+    a_guess = Along(T_GUESS, g.at[steps, mid], g.at[0, mid])
+    last_guess.wait()
+    a_guess.start()
     for flag, dev in ((has_up, up), (has_dn, dn)):
         @pl.when(jnp.logical_and(even_row, flag))
         def _(dev=dev):
             pl.semaphore_signal(ready, inc=1, device_id=dev, device_id_type=MESH)
-
-    a_guess = Along(T_GUESS, g.at[steps, mid], g.at[0, mid])
-    last_guess.wait()
-    a_guess.start()
 
     @pl.when(jnp.logical_and(odd_row, rows_beside > 0))
     def _():
@@ -192,9 +194,9 @@
         n = steps - i
         halo((i + 1) // 2, n - 1, guess_hbm, g)
         halo((i + 1) // 2, n, src_hbm, s)
+    for load in loaded:
+        load.wait()
     halo(half - 1, 1, src_hbm, s)
-    for load in loads:
-        load.wait()
 
     lane = lax.broadcasted_iota(jnp.int32, (full, LANES), 1)
     is_first, is_last = lane == 0, lane == LANES - 1
@@ -292,7 +294,7 @@
     def start_u3():
         u3_kept.start()
 
-        @pl.when(jnp.logical_not(jnp.logical_or(by_relay, by_hand)))
+        @pl.when(jnp.logical_not(jnp.logical_or(by_relay, handing)))
         def _():
             u3_rest.start()
 
@@ -313,6 +315,10 @@
     def forward(source, target):
         give(RELAY, T_RELAY, relay, relay, *source).wait_recv()
         give(RELAY, T_U3, relay, u3_rest.dst, *target).start()
+
+        @pl.when(handing)
+        def _():
+            u3_rest.start()
 
     def forwarded(source, target):
         give(RELAY, T_U3, relay, u3_rest.dst, *target).wait_send()
@@ -362,7 +368,7 @@
         start_g.wait()
         start_u.wait()
     a_guess.wait_recv()
-    f_guess = within(0, g, slice(0, 1))
+    f_guess = within(alone, g, slice(0, 1))
     f_guess.start()
     sweep_one(3, half + 1)
     each(4, half + 1, lambda m: coarse_defect(c1, m))
@@ -373,7 +379,7 @@
     a_e2.start()
     each(1, 2, lambda n: second_sweep(g, e, n, u1, w, damping))
     a_q.wait_recv()
-    f_q = within(1, s, slice(0, 1))
+    f_q = within(0, s, slice(0, 1))
     f_q.start()
     f_q.wait_recv()
     each(0, 1, lambda n: first_sweep(g, n, has_prev=False))
@@ -383,7 +389,7 @@
     each(1, 2, lambda m: second_sweep(None, er, m, c0, wk, damping))
     sweep_one(2, 3)
     sweep_two(3, 4)
-    x_late = within(0, c2, slice(3, half + 1))
+    x_late = within(1, c2, slice(3, half + 1))
     x_late.start()
     a_e0.wait_recv()
     f_e0 = within(2, c0, slice(0, 1))
@@ -401,7 +407,7 @@
     start_u3()
     each(1, 2, lambda m: second_sweep(c0, ec, m, c1, wk, damping))
     sweep_two(2, 3)
-    x_mid = within(1, c2, slice(2, 3))
+    x_mid = within(0, c2, slice(2, 3))
     x_mid.start()
     for j in range(chunks):
         u2[steps - 2, :, at(j)] = u1[steps - 2, :, at(j)] + c2[half - 1, :, at(j)]
@@ -411,7 +417,7 @@
     a_e1.rest.wait_recv()
     f_e1.wait_recv()
     sweep_two(1, 2)
-    x_early = within(0, c2, slice(1, 2))
+    x_early = within(1, c2, slice(1, 2))
     x_early.start()
     x_mid.wait_recv()
     each(3, half, prolong)
@@ -490,7 +496,7 @@
                 pltpu.VMEM((rows, cols), jnp.float32),
                 pltpu.VMEM((RELAYED, cols), jnp.float32),
                 pltpu.SemaphoreType.DMA((4,)),
-                pltpu.SemaphoreType.DMA((half + SETS + PARTS,)),
+                pltpu.SemaphoreType.DMA((half + 1 + PARTS,)),
                 pltpu.SemaphoreType.REGULAR,
             ],
             compiler_params=pltpu.CompilerParams(

time: 39.3 us -> 39.3 us (level)
  no operation moved by 1% of the time
where the time goes in v8:
time: 39.3 us; the launch traced here: 38.5 us
  Pallas kernels  37.9 us (96%)
  between operations  0.64 us (2%)
    pallas_call x1, Pallas kernels, shards(): pl.pallas_call(functools.partial(kernel, tms, spaces), out_shape=(buf(ste...  35.9 us
    pallas_call x1, Pallas kernels, shards(): pl.pallas_call(store, out_shape=(jax.ShapeDtypeStruct(source.shape, jnp.f...  2.03 us

profile of v8, /device:TPU:0, one launch (start us, length us, event | category | flops | bytes accessed | tf_op | source)
XLA Modules:
  0.0 38.5 jit_solution(1338477233456832668)
XLA Ops:
  0.6 35.9 %shard_map.59 = (f32[9,80,1024]{2,1,0:T(8,128)S(1)}, f32[8,64,1024]{2,1,0:T(8,128)S(1)}) custom-call(f32[8,64,1024]{2,1,0:T(8,128)} %src_hbm.1, f32[8,64,1024]{2,1,0:T(8,128)} %guess_hbm.1, f32[64,1024]{1,0:T(8,128)} %start_hbm.1, f32[64,1024]{1,0:T(8,128)} %cond_hbm.1), custom_call_target="tpu_custom_call" | custom-call | tf_op jit(solution)/shard_map/pallas_call | solution.py:486
  36.5 2.0 %shard_map.60 = (f32[8,64,1024]{2,1,0:T(8,128)}, f32[8,64,1024]{2,1,0:T(8,128)}) custom-call(f32[9,80,1024]{2,1,0:T(8,128)S(1)} %get-tuple-element.4.u3, f32[8,64,1024]{2,1,0:T(8,128)S(1)} %get-tuple-element.5.rbuf), custom_call_target="tpu_custom_call" | custom-call | tf_op jit(solution)/shard_map/pallas_call | solution.py:505

commit v9 on v8

--- a/solution.py
+++ b/solution.py
@@ -13,8 +13,8 @@
 LANES = 128
 
 EARLY, SPACE, ALONG, RELAY = range(4)
-T_GUESS, T_Q, T_E0, T_E1_RIM, T_E1, T_E2_RIM, T_E2, T_U3, T_RELAY = range(9)
-PLANES, PARTS = 6, 9
+T_GUESS, T_Q, T_E0, T_E1_RIM, T_E1, T_E2_RIM, T_E2, T_KEPT, T_U3, T_RELAY = range(10)
+PLANES, PARTS = 6, 10
 RELAYED = 3 * HALO
 
 
@@ -27,6 +27,12 @@
     z = lax.axis_index("space")
     has_up, has_dn = z > 0, z < spaces - 1
     has_before, has_after = t > 0, t < tms - 1
+    barrier = pltpu.get_barrier_semaphore()
+
+    @pl.when(has_before)
+    def _():
+        pl.semaphore_signal(barrier, inc=1, device_id={"tm": t - 1}, device_id_type=MESH)
+
     by_relay = jnp.logical_and(lax.rem(t, 2) == 1, t + 2 < tms)
     is_relay = jnp.logical_and(lax.rem(t, 2) == 1, t > 2)
     from_relay = jnp.logical_and(lax.rem(t, 2) == 0, jnp.logical_and(t > 0, t + 1 < tms))
@@ -127,9 +133,8 @@
             SPACE, turn, ref.at[sl, top_in], ref.at[sl, bot_in], ref.at[sl, top], ref.at[sl, bot],
             sl.stop - sl.start)
 
-    barrier = pltpu.get_barrier_semaphore()
     greeted = (
-        (has_before, {"tm": t - 1}), (is_relay, {"tm": t - 2}), (from_relay, {"tm": t + 1}),
+        (is_relay, {"tm": t - 2}), (from_relay, {"tm": t + 1}),
         (jnp.logical_and(odd_row, has_up), up), (jnp.logical_and(odd_row, has_dn), dn))
     for flag, dev in greeted:
         @pl.when(flag)
@@ -282,9 +287,8 @@
     a_e0 = Along(T_E0, c0.at[half, mid], c0.at[0, mid])
     a_e1 = Split(T_E1_RIM, c1)
     a_e2 = Split(T_E2_RIM, c2)
-    a_u3 = Along(T_U3, fu, fu)
     kept = rows - RELAYED
-    u3_kept = Along(T_U3, u3.at[steps, HALO : HALO + kept], fu.at[0:kept])
+    u3_kept = Along(T_KEPT, u3.at[steps, HALO : HALO + kept], fu.at[0:kept])
     u3_rest = Along(T_U3, u3.at[steps, HALO + kept : HALO + rows], fu.at[kept:rows])
 
     def give(sent, k, src, dst, step, row_step=0):
@@ -457,8 +461,9 @@
 
     @pl.when(has_before)
     def _():
-        a_u3.wait_recv()
-        rbuf[0] = rbuf[0] + fu[...]
+        for part, lines in ((u3_kept, slice(0, kept)), (u3_rest, slice(kept, rows))):
+            part.wait_recv()
+            rbuf[0, lines] = rbuf[0, lines] + fu[lines]
 
 
 def store(u3, rbuf, u_out, r_out, sem):

time: 39.3 us -> 39.3 us (level)
  no operation moved by 1% of the time
where the time goes in v9:
time: 39.3 us; the launch traced here: 38.5 us
  Pallas kernels  37.9 us (96%)
  between operations  0.64 us (2%)
    pallas_call x1, Pallas kernels, shards(): pl.pallas_call(functools.partial(kernel, tms, spaces), out_shape=(buf(ste...  35.9 us
    pallas_call x1, Pallas kernels, shards(): pl.pallas_call(store, out_shape=(jax.ShapeDtypeStruct(source.shape, jnp.f...  2.03 us

profile of v9, /device:TPU:0, one launch (start us, length us, event | category | flops | bytes accessed | tf_op | source)
XLA Modules:
  0.0 38.5 jit_solution(5062505340122232280)
XLA Ops:
  0.6 35.9 %shard_map.59 = (f32[9,80,1024]{2,1,0:T(8,128)S(1)}, f32[8,64,1024]{2,1,0:T(8,128)S(1)}) custom-call(f32[8,64,1024]{2,1,0:T(8,128)} %src_hbm.1, f32[8,64,1024]{2,1,0:T(8,128)} %guess_hbm.1, f32[64,1024]{1,0:T(8,128)} %start_hbm.1, f32[64,1024]{1,0:T(8,128)} %cond_hbm.1), custom_call_target="tpu_custom_call" | custom-call | tf_op jit(solution)/shard_map/pallas_call | solution.py:491
  36.5 2.0 %shard_map.60 = (f32[8,64,1024]{2,1,0:T(8,128)}, f32[8,64,1024]{2,1,0:T(8,128)}) custom-call(f32[9,80,1024]{2,1,0:T(8,128)S(1)} %get-tuple-element.4.u3, f32[8,64,1024]{2,1,0:T(8,128)S(1)} %get-tuple-element.5.rbuf), custom_call_target="tpu_custom_call" | custom-call | tf_op jit(solution)/shard_map/pallas_call | solution.py:510

commit v10 on v9

--- a/solution.py
+++ b/solution.py
@@ -15,7 +15,7 @@
 EARLY, SPACE, ALONG, RELAY = range(4)
 T_GUESS, T_Q, T_E0, T_E1_RIM, T_E1, T_E2_RIM, T_E2, T_KEPT, T_U3, T_RELAY = range(10)
 PLANES, PARTS = 6, 10
-RELAYED = 3 * HALO
+RELAYED = 4 * HALO
 
 
 def kernel(

time: 39.3 us -> 39.3 us (level)
  the two profiles are of different devices: /device:TPU:0 before, /device:TPU:1 now
where the time goes in v10:
time: 39.3 us; the launch traced here: 39.1 us
  Pallas kernels  38.5 us (98%)
  between operations  0.64 us (2%)
    pallas_call x1, Pallas kernels, shards(): pl.pallas_call(functools.partial(kernel, tms, spaces), out_shape=(buf(ste...  36.5 us
    pallas_call x1, Pallas kernels, shards(): pl.pallas_call(store, out_shape=(jax.ShapeDtypeStruct(source.shape, jnp.f...  2.03 us

profile of v10, /device:TPU:1, one launch (start us, length us, event | category | flops | bytes accessed | tf_op | source)
XLA Modules:
  0.0 39.1 jit_solution(14466652762615648166)
XLA Ops:
  0.6 36.5 %shard_map.59 = (f32[9,80,1024]{2,1,0:T(8,128)S(1)}, f32[8,64,1024]{2,1,0:T(8,128)S(1)}) custom-call(f32[8,64,1024]{2,1,0:T(8,128)} %src_hbm.1, f32[8,64,1024]{2,1,0:T(8,128)} %guess_hbm.1, f32[64,1024]{1,0:T(8,128)} %start_hbm.1, f32[64,1024]{1,0:T(8,128)} %cond_hbm.1), custom_call_target="tpu_custom_call" | custom-call | tf_op jit(solution)/shard_map/pallas_call | solution.py:491
  37.1 2.0 %shard_map.60 = (f32[8,64,1024]{2,1,0:T(8,128)}, f32[8,64,1024]{2,1,0:T(8,128)}) custom-call(f32[9,80,1024]{2,1,0:T(8,128)S(1)} %get-tuple-element.4.u3, f32[8,64,1024]{2,1,0:T(8,128)S(1)} %get-tuple-element.5.rbuf), custom_call_target="tpu_custom_call" | custom-call | tf_op jit(solution)/shard_map/pallas_call | solution.py:510

commit v11 on v10

--- a/solution.py
+++ b/solution.py
@@ -15,7 +15,7 @@
 EARLY, SPACE, ALONG, RELAY = range(4)
 T_GUESS, T_Q, T_E0, T_E1_RIM, T_E1, T_E2_RIM, T_E2, T_KEPT, T_U3, T_RELAY = range(10)
 PLANES, PARTS = 6, 10
-RELAYED = 4 * HALO
+RELAYED = 5 * HALO
 
 
 def kernel(

time: 39.3 us -> 39.3 us (level)
  no operation moved by 1% of the time
where the time goes in v11:
time: 39.3 us; the launch traced here: 39.1 us
  Pallas kernels  38.5 us (98%)
  between operations  0.64 us (2%)
    pallas_call x1, Pallas kernels, shards(): pl.pallas_call(functools.partial(kernel, tms, spaces), out_shape=(buf(ste...  36.5 us
    pallas_call x1, Pallas kernels, shards(): pl.pallas_call(store, out_shape=(jax.ShapeDtypeStruct(source.shape, jnp.f...  2.03 us

profile of v11, /device:TPU:1, one launch (start us, length us, event | category | flops | bytes accessed | tf_op | source)
XLA Modules:
  0.0 39.1 jit_solution(11424753601595501389)
XLA Ops:
  0.6 36.5 %shard_map.59 = (f32[9,80,1024]{2,1,0:T(8,128)S(1)}, f32[8,64,1024]{2,1,0:T(8,128)S(1)}) custom-call(f32[8,64,1024]{2,1,0:T(8,128)} %src_hbm.1, f32[8,64,1024]{2,1,0:T(8,128)} %guess_hbm.1, f32[64,1024]{1,0:T(8,128)} %start_hbm.1, f32[64,1024]{1,0:T(8,128)} %cond_hbm.1), custom_call_target="tpu_custom_call" | custom-call | tf_op jit(solution)/shard_map/pallas_call | solution.py:491
  37.1 2.0 %shard_map.60 = (f32[8,64,1024]{2,1,0:T(8,128)}, f32[8,64,1024]{2,1,0:T(8,128)}) custom-call(f32[9,80,1024]{2,1,0:T(8,128)S(1)} %get-tuple-element.4.u3, f32[8,64,1024]{2,1,0:T(8,128)S(1)} %get-tuple-element.5.rbuf), custom_call_target="tpu_custom_call" | custom-call | tf_op jit(solution)/shard_map/pallas_call | solution.py:510
